TPU v7x, 32 devices: a whole 2x2x4 slice. The times are simulated.
32 devices in a mesh: groups: 2 (over y), seq: 4 (over z), tp: 4 (over x, core).
Axes of the slice: x: 2, y: 2, z: 4, core: 2. Of those that a mesh axis runs over, the one named last changes fastest.
Arguments:
- resp_queries: bfloat16 [4096, 8192], P(('groups', 'seq'), 'tp'), parts along dimension 0, may hold values from -300 to 300
- resp_keys: bfloat16 [4096, 1024], P(('groups', 'seq'), 'tp'), parts along dimension 0, may hold values from -4 to 4
- resp_values: bfloat16 [4096, 1024], P(('groups', 'seq'), 'tp'), parts along dimension 0, may hold values from -48 to 48
- prompt_keys: bfloat16 [2048, 1024], P(('groups', 'seq'), 'tp'), parts along dimension 0, may hold values from -4 to 4
- prompt_values: bfloat16 [2048, 1024], P(('groups', 'seq'), 'tp'), parts along dimension 0, may hold values from -48 to 48
- out_weight: bfloat16 [8192, 8192], P('tp', 'seq'), may hold values from -0.0625 to 0.0625
- resp_blocks: int32 [8], P('groups'), parts along dimension 0, may hold values from 1 to 4, 11 in all
Outputs:
- attended: bfloat16 [4096, 8192], P(('groups', 'seq'), 'tp'), parts along dimension 0
There are 2 independent parts, one for each index of `groups`. A program takes and returns all parts, laid end to end along the dimension named above; an argument that names none is the same for every part. Nothing has to cross between parts.
Inputs may be any that keep to these rules, and one draw needn't show every extreme that they name: `resp_blocks`: the lengths sum to 11 blocks and the longest is exactly 4 blocks.
All inputs are finite; a program needn't handle non-finite values.
Results may differ from a plain program's by a relative error of at most 0.017.
Values may be sent and summed in bfloat16 or wider, within the bound.
A program may use at most 128 MiB of HBM per device.

v0:
```python
import functools
import jax
import jax.numpy as jnp
from jax import lax
from jax.experimental import pallas as pl
from jax.experimental.pallas import tpu as pltpu
from jax.sharding import PartitionSpec as P

HD = 128
BLOCK = 128
MAXB = 4
LOG2E = 1.4426950408889634


def attend_block(q, kp, vp, kr, vr, first, rows):
    c = (HD ** -0.5) * LOG2E
    nt = (((1,), (1,)), ((), ()))
    sp = lax.dot_general(q, kp, nt, preferred_element_type=jnp.float32)
    sr = lax.dot_general(q, kr, nt, preferred_element_type=jnp.float32)
    qpos = lax.broadcasted_iota(jnp.int32, sr.shape, 0) % rows + first
    kpos = lax.broadcasted_iota(jnp.int32, sr.shape, 1)
    sr = jnp.where(kpos <= qpos, sr, -1e30)
    m = jnp.maximum(
        jnp.max(sp, axis=1, keepdims=True), jnp.max(sr, axis=1, keepdims=True)
    )
    ep = jnp.exp2((sp - m) * c)
    er = jnp.exp2((sr - m) * c)
    total = jnp.sum(ep, axis=1, keepdims=True) + jnp.sum(er, axis=1, keepdims=True)
    acc = jnp.dot(ep.astype(jnp.bfloat16), vp, preferred_element_type=jnp.float32)
    acc = acc + jnp.dot(er.astype(jnp.bfloat16), vr, preferred_element_type=jnp.float32)
    return (acc / total).astype(jnp.bfloat16)


MESH = pl.DeviceIdType.MESH


def fused_kernel(
    nseq, ntp, group,
    lens_ref, q_ref, kr_ref, vr_ref, pkv_ref, w_ref, out_ref,
    prompt, gath, part, half_in, quart_in, final,
    p_send, p_recv, g_send, g_recv, a_send, a_recv, b_send, b_recv, f_send, f_recv,
):
    s = lax.axis_index("seq")
    t = lax.axis_index("tp")
    core, x = lax.rem(t, 2), lax.div(t, 2)
    partner = t + 1 - 2 * core
    nx = ntp // 2
    per = nseq // ntp
    chunks = nseq * MAXB
    prows = pkv_ref.shape[0]
    cols = w_ref.shape[1]
    half = BLOCK // 2
    quart = half // nx
    kv_local = kr_ref.shape[1] // HD
    has_right, has_left = s < nseq - 1, s > 0
    home = lax.div(s, per)
    slab = lax.rem(s, per)

    def p_copy(r, side):
        return pltpu.make_async_remote_copy(
            src_ref=prompt.at[pl.ds(r * prows, prows)],
            dst_ref=prompt.at[pl.ds(r * prows, prows)],
            send_sem=p_send.at[side, r],
            recv_sem=p_recv.at[r],
            device_id={"seq": s - 1 + 2 * side},
            device_id_type=MESH,
        )

    def g_copy(r, b, side):
        return pltpu.make_async_remote_copy(
            src_ref=gath.at[r, b],
            dst_ref=gath.at[r, b],
            send_sem=g_send.at[side, r, b],
            recv_sem=g_recv.at[r, b],
            device_id={"seq": s - 1 + 2 * side},
            device_id_type=MESH,
        )

    def a_copy(i):
        return pltpu.make_async_remote_copy(
            src_ref=part.at[i, pl.ds((1 - core) * half, half)],
            dst_ref=half_in.at[i],
            send_sem=a_send.at[i],
            recv_sem=a_recv.at[i],
            device_id={"tp": partner},
            device_id_type=MESH,
        )

    def b_copy(i, k):
        other = lax.rem(x + k, nx)
        return pltpu.make_async_remote_copy(
            src_ref=part.at[i, pl.ds(core * half + other * quart, quart)],
            dst_ref=quart_in.at[i, k - 1],
            send_sem=b_send.at[i, k - 1],
            recv_sem=b_recv.at[i, k - 1],
            device_id={"tp": other * 2 + core},
            device_id_type=MESH,
        )

    def f_copy(i, r, b):
        return pltpu.make_async_remote_copy(
            src_ref=final.at[i],
            dst_ref=out_ref.at[slab, pl.ds(b * BLOCK + core * half + x * quart, quart)],
            send_sem=f_send.at[i],
            recv_sem=f_recv.at[b, slab, t],
            device_id={"seq": r, "tp": home},
            device_id_type=MESH,
        )

    both = jnp.minimum(s, nseq - 1 - s)
    far_side = jnp.where(s > nseq - 1 - s, -1, 1)

    def chunk_of(i):
        j = jnp.maximum(i - MAXB, 0)
        twin = 2 * MAXB
        jj = jnp.maximum(j - twin * both, 0)
        near = j < twin * both
        d = jnp.where(near, lax.div(j, twin) + 1, both + 1 + lax.div(jj, MAXB))
        b = jnp.where(near, lax.div(lax.rem(j, twin), 2), lax.rem(jj, MAXB))
        side = jnp.where(near, 2 * lax.rem(j, 2) - 1, far_side)
        own = i < MAXB
        return jnp.where(own, s, s + side * d), jnp.where(own, i, b)

    def loop(n, fn, start=0):
        def step(i, carry):
            fn(i)
            return carry

        lax.fori_loop(start, n, step, 0)

    prompt[pl.ds(s * prows, prows), :] = pkv_ref[...]

    @pl.when(has_left)
    def _():
        p_copy(s, 0).start()

    @pl.when(has_right)
    def _():
        p_copy(s, 1).start()

    def gather_prompt(d):
        @pl.when(s - d >= 0)
        def _():
            p_copy(s - d, 1).wait_recv()

            @pl.when(has_right)
            def _():
                p_copy(s - d, 1).start()

        @pl.when(s + d < nseq)
        def _():
            p_copy(s + d, 0).wait_recv()

            @pl.when(has_left)
            def _():
                p_copy(s + d, 0).start()

    loop(nseq, gather_prompt, 1)

    def stage_a(i):
        r, b = chunk_of(i)

        @pl.when(i < MAXB)
        def _():
            first = i * BLOCK
            run = max(group // 2, 1)
            for k in range(kv_local):
                kcol = slice(k * HD, (k + 1) * HD)
                vcol = slice((kv_local + k) * HD, (kv_local + k + 1) * HD)
                for h in range(k * group, (k + 1) * group, run):
                    q = jnp.concatenate(
                        [
                            q_ref[pl.ds(first, BLOCK), (h + g) * HD : (h + g + 1) * HD]
                            for g in range(run)
                        ],
                        axis=0,
                    )
                    o = attend_block(
                        q, prompt[:, kcol], prompt[:, vcol], kr_ref[:, kcol], vr_ref[:, kcol],
                        first, BLOCK,
                    )
                    for g in range(run):
                        gath[s, i, :, (h + g) * HD : (h + g + 1) * HD] = o[
                            g * BLOCK : (g + 1) * BLOCK
                        ]

        @pl.when(i >= MAXB)
        def _():
            g_copy(r, b, 0).wait_recv()

        @pl.when(has_right & (r <= s))
        def _():
            g_copy(r, b, 1).start()

        @pl.when(has_left & (r >= s))
        def _():
            g_copy(r, b, 0).start()

        part[i] = jnp.dot(
            gath[r, b], w_ref[...], preferred_element_type=jnp.float32
        ).astype(jnp.bfloat16)
        a_copy(i).start()

    def stage_b(i):
        a_copy(i).wait_recv()
        mine = pl.ds(core * half, half)
        part[i, mine, :] = (
            part[i, mine, :].astype(jnp.float32) + half_in[i].astype(jnp.float32)
        ).astype(jnp.bfloat16)
        for k in range(1, nx):
            b_copy(i, k).start()

    def stage_c(i):
        r, b = chunk_of(i)
        for k in range(1, nx):
            b_copy(i, k).wait_recv()
        total = part[i, pl.ds(core * half + x * quart, quart), :].astype(jnp.float32)
        for k in range(1, nx):
            total = total + quart_in[i, k - 1].astype(jnp.float32)
        row = lax.broadcasted_iota(jnp.int32, total.shape, 0)
        row = row + (b * BLOCK + core * half + x * quart)
        total = jnp.where(row < lens_ref[r] * BLOCK, total, 0.0)
        final[i] = total.astype(jnp.bfloat16)
        here = (r == s) & (home == t)

        @pl.when(here)
        def _():
            out_ref[slab, pl.ds(b * BLOCK + core * half + x * quart, quart), :] = final[i]

        @pl.when(jnp.logical_not(here))
        def _():
            f_copy(i, r, b).start()

    def step(i):
        @pl.when(i < chunks)
        def _():
            stage_a(i)

        @pl.when((i >= 1) & (i < chunks + 1))
        def _():
            stage_b(i - 1)

        @pl.when(i >= 2)
        def _():
            stage_c(i - 2)

    loop(chunks + 2, step)

    def drain_send(i):
        r, b = chunk_of(i)

        @pl.when(has_right & (r <= s))
        def _():
            g_copy(r, b, 1).wait_send()

        @pl.when(has_left & (r >= s))
        def _():
            g_copy(r, b, 0).wait_send()

        a_copy(i).wait_send()
        for k in range(1, nx):
            b_copy(i, k).wait_send()

        @pl.when(jnp.logical_not((r == s) & (home == t)))
        def _():
            f_copy(i, r, b).wait_send()

    loop(chunks, drain_send)

    def drain_prompt(r):
        @pl.when(has_right & (r <= s))
        def _():
            p_copy(r, 1).wait_send()

        @pl.when(has_left & (r >= s))
        def _():
            p_copy(r, 0).wait_send()

    loop(nseq, drain_prompt)

    def drain_out(m):
        b = lax.div(m, per * ntp)
        j = lax.div(lax.rem(m, per * ntp), ntp)
        u = lax.rem(m, ntp)

        @pl.when(jnp.logical_not((t * per + j == s) & (u == t)))
        def _():
            row = b * BLOCK + lax.rem(u, 2) * half + lax.div(u, 2) * quart
            pltpu.make_async_remote_copy(
                src_ref=final.at[0],
                dst_ref=out_ref.at[j, pl.ds(row, quart)],
                send_sem=f_send.at[0],
                recv_sem=f_recv.at[b, j, u],
                device_id={"seq": s, "tp": partner},
                device_id_type=MESH,
            ).wait_recv()

    loop(MAXB * per * ntp, drain_out)


def per_device(
    resp_queries, resp_keys, resp_values, prompt_keys, prompt_values, out_weight, resp_blocks
):
    nseq = lax.axis_size("seq")
    ntp = lax.axis_size("tp")
    rows, depth = resp_queries.shape
    assert rows == MAXB * BLOCK and nseq % ntp == 0 and ntp % 2 == 0
    nx, per, chunks = ntp // 2, nseq // ntp, nseq * MAXB
    cols = out_weight.shape[1]
    pkv = jnp.concatenate([prompt_keys, prompt_values], axis=1)
    quart = BLOCK // ntp
    bf = jnp.bfloat16
    dma = pltpu.SemaphoreType.DMA
    vmem = pl.BlockSpec(memory_space=pltpu.VMEM)
    out = pl.pallas_call(
        functools.partial(fused_kernel, nseq, ntp, depth // resp_keys.shape[1]),
        out_shape=jax.ShapeDtypeStruct((per, rows, cols), bf),
        in_specs=[pl.BlockSpec(memory_space=pltpu.SMEM)] + [vmem] * 5,
        out_specs=vmem,
        scratch_shapes=[
            pltpu.VMEM((nseq * pkv.shape[0], pkv.shape[1]), bf),
            pltpu.VMEM((nseq, MAXB, BLOCK, depth), bf),
            pltpu.VMEM((chunks, BLOCK, cols), bf),
            pltpu.VMEM((chunks, BLOCK // 2, cols), bf),
            pltpu.VMEM((chunks, max(nx - 1, 1), quart, cols), bf),
            pltpu.VMEM((chunks, quart, cols), bf),
            dma((2, nseq)),
            dma((nseq,)),
            dma((2, nseq, MAXB)),
            dma((nseq, MAXB)),
            dma((chunks,)),
            dma((chunks,)),
            dma((chunks, max(nx - 1, 1))),
            dma((chunks, max(nx - 1, 1))),
            dma((chunks,)),
            dma((MAXB, per, ntp)),
        ],
        compiler_params=pltpu.CompilerParams(
            has_side_effects=True, vmem_limit_bytes=61000 * 1024
        ),
    )(resp_blocks, resp_queries, resp_keys, resp_values, pkv, out_weight)
    return out.transpose(1, 0, 2).reshape(rows, per * cols)


def solution(mesh):
    return jax.shard_map(
        per_device,
        mesh=mesh,
        in_specs=(
            P(("groups", "seq"), "tp"),
            P(("groups", "seq"), "tp"),
            P(("groups", "seq"), "tp"),
            P(("groups", "seq"), "tp"),
            P(("groups", "seq"), "tp"),
            P("tp", "seq"),
            P("groups"),
        ),
        out_specs=P(("groups", "seq"), "tp"),
        check_vma=False,
    )
```

profile of v0, /device:TPU:28, one launch (start us, length us, event | category | flops | bytes accessed | tf_op | source)
XLA Modules:
  0.0 221.0 jit_solution(11422493611140517097)
XLA Ops:
  0.0 1.7 pad_maximum_fusion.pkv_ref
  1.7 216.1 %shard_map.73 = bf16[1,512,2048]{2,1,0:T(8,128)(2,1)} custom-call(s32[4]{0:T(128)} %lens_ref.1, bf16[512,2048]{1,0:T(8,128)(2,1)} %q_ref.1, bf16[512,256]{1,0:T(8,128)(2,1)} %kr_ref.1, bf16[512,256]{1,0:T(8,128)(2,1)} %vr_ref.1, bf16[256,512]{1,0:T(8,128)(2,1)} %pad_maximum_fusion.pkv_ref, bf16[2048,2048]{1,0:T(8,128)(2,1)} %w_ref.1), custom_call_target="tpu_custom_call" | custom-call | tf_op jit(solution)/shard_map/pallas_call | solution.py:315
  217.8 3.2 %copy.9 = bf16[512,2048]{1,0:T(8,128)(2,1)} copy(bf16[512,2048]{1,0:T(8,128)(2,1)} %bitcast.1) | data formatting | bytes 4194304
where the time goes:
time: 221 us
  Pallas kernels  216 us (98%)
  local copies, waits for them, and re-layouts  3.16 us (1%)
    pallas_call x1, Pallas kernels, per_device(): pl.pallas_call(functools.partial(fused_kernel, nseq, ntp, depth // resp_k...  216 us

commit v1 on v0

v1 whole, which is shorter than its diff:
```python
import functools
import jax
import jax.numpy as jnp
from jax import lax
from jax.experimental import pallas as pl
from jax.experimental.pallas import tpu as pltpu
from jax.sharding import PartitionSpec as P

HD = 128
BLOCK = 128
MAXB = 4
LOG2E = 1.4426950408889634


def attend_block(q, kp, vp, kr, vr, first, rows):
    c = (HD ** -0.5) * LOG2E
    nt = (((1,), (1,)), ((), ()))
    sp = lax.dot_general(q, kp, nt, preferred_element_type=jnp.float32)
    sr = lax.dot_general(q, kr, nt, preferred_element_type=jnp.float32)
    qpos = lax.broadcasted_iota(jnp.int32, sr.shape, 0) % rows + first
    kpos = lax.broadcasted_iota(jnp.int32, sr.shape, 1)
    sr = jnp.where(kpos <= qpos, sr, -1e30)
    m = jnp.maximum(
        jnp.max(sp, axis=1, keepdims=True), jnp.max(sr, axis=1, keepdims=True)
    )
    ep = jnp.exp2((sp - m) * c)
    er = jnp.exp2((sr - m) * c)
    total = jnp.sum(ep, axis=1, keepdims=True) + jnp.sum(er, axis=1, keepdims=True)
    acc = jnp.dot(ep.astype(jnp.bfloat16), vp, preferred_element_type=jnp.float32)
    acc = acc + jnp.dot(er.astype(jnp.bfloat16), vr, preferred_element_type=jnp.float32)
    return (acc / total).astype(jnp.bfloat16)


MESH = pl.DeviceIdType.MESH
WPIECES = 4
NTILE = 512
SCORES = 1 << 20
MLAG_A = MAXB + 1
MLAG_C = MAXB + 5


def fused_kernel(
    nseq, ntp, group,
    lens_ref, q_ref, kr_ref, vr_ref, pk_ref, pv_ref, w_hbm, out_ref,
    pk_all, pv_all, w_ref, wm, ga, gb, part, half_in, quart_in, mig_in,
    p_send, p_recv, w_sem, wm_send, wm_recv, g_send, g_recv,
    a_send, a_recv, b_send, b_recv, f_send, f_recv, m_recv,
):
    s = lax.axis_index("seq")
    t = lax.axis_index("tp")
    core, x = lax.rem(t, 2), lax.div(t, 2)
    partner = t + 1 - 2 * core
    nx = ntp // 2
    per = nseq // ntp
    last = nseq - 1
    chunks = nseq * MAXB
    nmig = last * MAXB
    prows = pk_ref.shape[0]
    depth, cols = w_ref.shape
    mig = wm.shape[0]
    half = BLOCK // 2
    quart = half // nx
    my_quart = pl.ds(core * half + x * quart, quart)
    kv_local = kr_ref.shape[1] // HD
    has_right, has_left = s < last, s > 0
    is_end = (s == 0) | (s == last)
    is_pre = (s == 1) | (s == last - 1)
    end = jnp.where(s < nseq // 2, 0, last)
    inward = jnp.where(s < nseq // 2, 1, -1)

    def p_copy(r, side, kv, own=False):
        dst = (pk_all, pv_all)[kv]
        src = (pk_ref, pv_ref)[kv] if own else dst.at[pl.ds(r * prows, prows)]
        return pltpu.make_async_remote_copy(
            src_ref=src,
            dst_ref=dst.at[pl.ds(r * prows, prows)],
            send_sem=p_send.at[side, r, kv],
            recv_sem=p_recv.at[r, kv],
            device_id={"seq": s - 1 + 2 * side},
            device_id_type=MESH,
        )

    def w_local(k):
        rows = pl.ds(k * (depth // WPIECES), depth // WPIECES)
        return pltpu.make_async_copy(w_hbm.at[rows], w_ref.at[rows], w_sem.at[k])

    def w_copy(k):
        rows = pl.ds(k * (mig // WPIECES), mig // WPIECES)
        return pltpu.make_async_remote_copy(
            src_ref=w_hbm.at[rows],
            dst_ref=wm.at[rows],
            send_sem=wm_send.at[k],
            recv_sem=wm_recv.at[k],
            device_id={"seq": jnp.where(is_end, s + inward, end)},
            device_id_type=MESH,
        )

    def g_copy(h, r, b, side):
        buf = (ga, gb)[h]
        return pltpu.make_async_remote_copy(
            src_ref=buf.at[r, b],
            dst_ref=buf.at[r, b],
            send_sem=g_send.at[h, side, r, b],
            recv_sem=g_recv.at[h, r, b],
            device_id={"seq": s - 1 + 2 * side},
            device_id_type=MESH,
        )

    def a_copy(i):
        return pltpu.make_async_remote_copy(
            src_ref=part.at[i, pl.ds((1 - core) * half, half)],
            dst_ref=half_in.at[i],
            send_sem=a_send.at[i],
            recv_sem=a_recv.at[i],
            device_id={"tp": partner},
            device_id_type=MESH,
        )

    def b_copy(i, k):
        other = lax.rem(x + k, nx)
        return pltpu.make_async_remote_copy(
            src_ref=part.at[i, pl.ds(core * half + other * quart, quart)],
            dst_ref=quart_in.at[i, k - 1],
            send_sem=b_send.at[i, k - 1],
            recv_sem=b_recv.at[i, k - 1],
            device_id={"tp": other * 2 + core},
            device_id_type=MESH,
        )

    def row_of(b):
        return b * BLOCK + core * half + x * quart

    def f_copy(i, r, b, owner):
        home, slab = lax.div(owner, per), lax.rem(owner, per)
        return pltpu.make_async_remote_copy(
            src_ref=part.at[i, my_quart],
            dst_ref=out_ref.at[slab, pl.ds(row_of(b), quart)],
            send_sem=f_send.at[i],
            recv_sem=f_recv.at[b, slab, t],
            device_id={"seq": r, "tp": home},
            device_id_type=MESH,
        )

    def m_copy(i, m):
        return pltpu.make_async_remote_copy(
            src_ref=part.at[i, my_quart],
            dst_ref=mig_in.at[m],
            send_sem=f_send.at[i],
            recv_sem=m_recv.at[m],
            device_id={"seq": jnp.where(is_end, s + inward, end)},
            device_id_type=MESH,
        )

    both = jnp.minimum(s, last - s)
    far_side = jnp.where(s > last - s, -1, 1)

    def chunk_of(i):
        j = jnp.maximum(i - MAXB, 0)
        twin = 2 * MAXB
        jj = jnp.maximum(j - twin * both, 0)
        near = j < twin * both
        d = jnp.where(near, lax.div(j, twin) + 1, both + 1 + lax.div(jj, MAXB))
        b = jnp.where(near, lax.div(lax.rem(j, twin), 2), lax.rem(jj, MAXB))
        side = jnp.where(near, 2 * lax.rem(j, 2) - 1, far_side)
        own = i < MAXB
        return jnp.where(own, s, s + side * d), jnp.where(own, i, b)

    def mig_of(m):
        return end + inward * (1 + lax.div(m, MAXB)), lax.rem(m, MAXB)

    def loop(n, fn, start=0):
        def step(i, carry):
            fn(i)
            return carry

        lax.fori_loop(start, n, step, 0)

    def goes(h, r, side):
        if side:
            ok = has_right & (r <= s)
            return ok & (s + 1 < last) if h == 0 else ok
        ok = has_left & (r >= s)
        return ok & (s > 1) if h == 0 else ok

    def send(h, r, b):
        for side in (1, 0):
            @pl.when(goes(h, r, side))
            def _():
                g_copy(h, r, b, side).start()

    for side, ok in ((0, has_left), (1, has_right)):
        @pl.when(ok)
        def _():
            p_copy(s, side, 0, own=True).start()
            p_copy(s, side, 1, own=True).start()

    @pl.when(is_end)
    def _():
        for k in range(WPIECES):
            w_copy(k).start()

    for k in range(WPIECES):
        w_local(k).start()

    pk_all[pl.ds(s * prows, prows), :] = pk_ref[...]
    pv_all[pl.ds(s * prows, prows), :] = pv_ref[...]

    def gather_prompt(d):
        for ok, r, side, onward in (
            (s - d >= 0, s - d, 1, has_right),
            (s + d < nseq, s + d, 0, has_left),
        ):
            @pl.when(ok)
            def _():
                for kv in range(2):
                    p_copy(r, side, kv).wait_recv()

                    @pl.when(onward)
                    def _():
                        p_copy(r, side, kv).start()

    loop(nseq, gather_prompt, 1)

    def project(i, r, b, full):
        @pl.when(full)
        def _():
            def tile(j):
                c = pl.ds(pl.multiple_of(j * NTILE, NTILE), NTILE)
                y = jnp.dot(ga[r, b], w_ref[:mig, c], preferred_element_type=jnp.float32)
                y = y + jnp.dot(gb[r, b], w_ref[mig:, c], preferred_element_type=jnp.float32)
                part[i, :, c] = y.astype(jnp.bfloat16)

            loop(cols // NTILE, tile)

        @pl.when(jnp.logical_not(full))
        def _():
            def tile(j):
                c = pl.ds(pl.multiple_of(j * NTILE, NTILE), NTILE)
                y = jnp.dot(gb[r, b], w_ref[mig:, c], preferred_element_type=jnp.float32)
                part[i, :, c] = y.astype(jnp.bfloat16)

            loop(cols // NTILE, tile)

        a_copy(i).start()

    def stage_a(i):
        r, b = chunk_of(i)

        @pl.when(i < MAXB)
        def _():
            first = i * BLOCK
            run = max(group // 2, 1)
            while run % 2 == 0 and run * BLOCK * pk_all.shape[0] > SCORES:
                run //= 2
            sent = False
            for k in range(kv_local):
                kvc = slice(k * HD, (k + 1) * HD)
                for h in range(k * group, (k + 1) * group, run):
                    q = jnp.concatenate(
                        [
                            q_ref[pl.ds(first, BLOCK), (h + g) * HD : (h + g + 1) * HD]
                            for g in range(run)
                        ],
                        axis=0,
                    )
                    o = attend_block(
                        q, pk_all[:, kvc], pv_all[:, kvc], kr_ref[:, kvc], vr_ref[:, kvc],
                        first, BLOCK,
                    )
                    for g in range(run):
                        at = (h + g) * HD
                        y = o[g * BLOCK : (g + 1) * BLOCK]
                        if at < mig:
                            ga[s, i, :, at : at + HD] = y
                        else:
                            gb[s, i, :, at - mig : at - mig + HD] = y
                    if not sent and (h + run) * HD >= mig:
                        sent = True
                        send(0, s, i)
            send(1, s, i)

        @pl.when(i >= MAXB)
        def _():
            @pl.when(jnp.logical_not(is_end))
            def _():
                g_copy(0, r, b, 0).wait_recv()

            send(0, r, b)
            g_copy(1, r, b, 0).wait_recv()
            send(1, r, b)

        @pl.when(i == 0)
        def _():
            for k in range(WPIECES):
                w_local(k).wait()

        project(i, r, b, (i < MAXB) | jnp.logical_not(is_end))

    def stage_b(i):
        a_copy(i).wait_recv()
        mine = pl.ds(core * half, half)
        part[i, mine, :] = (
            part[i, mine, :].astype(jnp.float32) + half_in[i].astype(jnp.float32)
        ).astype(jnp.bfloat16)
        for k in range(1, nx):
            b_copy(i, k).start()

    def reduced(i):
        for k in range(1, nx):
            b_copy(i, k).wait_recv()
        total = part[i, my_quart, :].astype(jnp.float32)
        for k in range(1, nx):
            total = total + quart_in[i, k - 1].astype(jnp.float32)
        return total

    def live(total, r, b):
        row = lax.broadcasted_iota(jnp.int32, total.shape, 0) + row_of(b)
        return jnp.where(row < lens_ref[r] * BLOCK, total, 0.0).astype(jnp.bfloat16)

    def stays(r, owner):
        return (r == s) & (lax.div(owner, per) == t)

    def deliver(i, r, b, owner):
        here = stays(r, owner)

        @pl.when(here)
        def _():
            out_ref[lax.rem(owner, per), pl.ds(row_of(b), quart), :] = part[i, my_quart, :]

        @pl.when(jnp.logical_not(here))
        def _():
            f_copy(i, r, b, owner).start()

    def hands_over(r):
        return is_end & (r != s)

    def stage_c(i):
        r, b = chunk_of(i)
        total = reduced(i)

        @pl.when(hands_over(r))
        def _():
            part[i, my_quart, :] = total.astype(jnp.bfloat16)
            m_copy(i, i - MAXB).start()

        @pl.when(jnp.logical_not(hands_over(r)))
        def _():
            part[i, my_quart, :] = live(total, r, b)
            deliver(i, r, b, s)

    def mig_a(m):
        r, b = mig_of(m)
        i = chunks + m

        @pl.when(m == 0)
        def _():
            for k in range(WPIECES):
                w_copy(k).wait_recv()

        def tile(j):
            c = pl.ds(pl.multiple_of(j * NTILE, NTILE), NTILE)
            y = jnp.dot(ga[r, b], wm[:, c], preferred_element_type=jnp.float32)
            part[i, :, c] = y.astype(jnp.bfloat16)

        loop(cols // NTILE, tile)
        a_copy(i).start()

    def mig_c(m):
        r, b = mig_of(m)
        i = chunks + m
        total = reduced(i)
        m_copy(i, m).wait_recv()
        part[i, my_quart, :] = live(total + mig_in[m].astype(jnp.float32), r, b)
        deliver(i, r, b, end)

    def step(i):
        @pl.when(i < chunks)
        def _():
            stage_a(i)

        @pl.when((i >= 1) & (i < chunks + 1))
        def _():
            stage_b(i - 1)

        @pl.when((i >= 2) & (i < chunks + 2))
        def _():
            stage_c(i - 2)

        @pl.when(is_pre & (i >= MLAG_A) & (i < MLAG_A + nmig))
        def _():
            mig_a(i - MLAG_A)

        @pl.when(is_pre & (i >= MLAG_A + 1) & (i < MLAG_A + 1 + nmig))
        def _():
            stage_b(chunks + i - MLAG_A - 1)

        @pl.when(is_pre & (i >= MLAG_C) & (i < MLAG_C + nmig))
        def _():
            mig_c(i - MLAG_C)

    loop(max(chunks + 2, MLAG_C + nmig), step)

    def drain_send(i):
        r, b = chunk_of(i)
        for h in range(2):
            for side in (1, 0):
                @pl.when(goes(h, r, side) & ((r == s) | jnp.logical_not(is_end)))
                def _():
                    g_copy(h, r, b, side).wait_send()

        a_copy(i).wait_send()
        for k in range(1, nx):
            b_copy(i, k).wait_send()

        @pl.when(hands_over(r))
        def _():
            m_copy(i, i - MAXB).wait_send()

        @pl.when(jnp.logical_not(hands_over(r) | stays(r, s)))
        def _():
            f_copy(i, r, b, s).wait_send()

    loop(chunks, drain_send)

    @pl.when(is_pre)
    def _():
        def drain_mig(m):
            r, b = mig_of(m)
            i = chunks + m
            a_copy(i).wait_send()
            for k in range(1, nx):
                b_copy(i, k).wait_send()

            @pl.when(jnp.logical_not(stays(r, end)))
            def _():
                f_copy(i, r, b, end).wait_send()

        loop(nmig, drain_mig)

    @pl.when(is_end)
    def _():
        for k in range(WPIECES):
            w_copy(k).wait_send()

    def drain_prompt(r):
        for kv in range(2):
            @pl.when(has_right & (r <= s))
            def _():
                p_copy(r, 1, kv).wait_send()

            @pl.when(has_left & (r >= s))
            def _():
                p_copy(r, 0, kv).wait_send()

    loop(nseq, drain_prompt)

    def drain_out(m):
        b = lax.div(m, per * ntp)
        j = lax.div(lax.rem(m, per * ntp), ntp)
        u = lax.rem(m, ntp)
        owner = t * per + j
        far = owner != s
        origin = jnp.where(far & (owner == 0), 1, jnp.where(far & (owner == last), last - 1, owner))

        @pl.when(jnp.logical_not((origin == s) & (u == t)))
        def _():
            row = b * BLOCK + lax.rem(u, 2) * half + lax.div(u, 2) * quart
            pltpu.make_async_remote_copy(
                src_ref=part.at[0, my_quart],
                dst_ref=out_ref.at[j, pl.ds(row, quart)],
                send_sem=f_send.at[0],
                recv_sem=f_recv.at[b, j, u],
                device_id={"seq": s, "tp": partner},
                device_id_type=MESH,
            ).wait_recv()

    loop(MAXB * per * ntp, drain_out)


def per_device(
    resp_queries, resp_keys, resp_values, prompt_keys, prompt_values, out_weight, resp_blocks
):
    nseq = lax.axis_size("seq")
    ntp = lax.axis_size("tp")
    rows, depth = resp_queries.shape
    assert rows == MAXB * BLOCK and nseq % ntp == 0 and ntp % 2 == 0 and nseq >= 4
    nx, per, chunks = ntp // 2, nseq // ntp, nseq * MAXB
    nmig = (nseq - 1) * MAXB
    every = chunks + nmig
    cols = out_weight.shape[1]
    mig = depth // HD // 4 * HD
    prows, kvw = prompt_keys.shape
    quart = BLOCK // ntp
    bf = jnp.bfloat16
    dma = pltpu.SemaphoreType.DMA
    vmem = pl.BlockSpec(memory_space=pltpu.VMEM)
    out = pl.pallas_call(
        functools.partial(fused_kernel, nseq, ntp, depth // resp_keys.shape[1]),
        out_shape=jax.ShapeDtypeStruct((per, rows, cols), bf),
        in_specs=[pl.BlockSpec(memory_space=pltpu.SMEM)]
        + [vmem] * 5
        + [pl.BlockSpec(memory_space=pl.ANY)],
        out_specs=vmem,
        scratch_shapes=[
            pltpu.VMEM((nseq * prows, kvw), bf),
            pltpu.VMEM((nseq * prows, kvw), bf),
            pltpu.VMEM((depth, cols), bf),
            pltpu.VMEM((mig, cols), bf),
            pltpu.VMEM((nseq, MAXB, BLOCK, mig), bf),
            pltpu.VMEM((nseq, MAXB, BLOCK, depth - mig), bf),
            pltpu.VMEM((every, BLOCK, cols), bf),
            pltpu.VMEM((every, BLOCK // 2, cols), bf),
            pltpu.VMEM((every, max(nx - 1, 1), quart, cols), bf),
            pltpu.VMEM((nmig, quart, cols), bf),
            dma((2, nseq, 2)),
            dma((nseq, 2)),
            dma((WPIECES,)),
            dma((WPIECES,)),
            dma((WPIECES,)),
            dma((2, 2, nseq, MAXB)),
            dma((2, nseq, MAXB)),
            dma((every,)),
            dma((every,)),
            dma((every, max(nx - 1, 1))),
            dma((every, max(nx - 1, 1))),
            dma((every,)),
            dma((MAXB, per, ntp)),
            dma((nmig,)),
        ],
        compiler_params=pltpu.CompilerParams(
            has_side_effects=True, vmem_limit_bytes=61000 * 1024
        ),
    )(resp_blocks, resp_queries, resp_keys, resp_values, prompt_keys, prompt_values, out_weight)
    return out.transpose(1, 0, 2).reshape(rows, per * cols)


def solution(mesh):
    return jax.shard_map(
        per_device,
        mesh=mesh,
        in_specs=(
            P(("groups", "seq"), "tp"),
            P(("groups", "seq"), "tp"),
            P(("groups", "seq"), "tp"),
            P(("groups", "seq"), "tp"),
            P(("groups", "seq"), "tp"),
            P("tp", "seq"),
            P("groups"),
        ),
        out_specs=P(("groups", "seq"), "tp"),
        check_vma=False,
    )
```

time: 221 us -> 199 us (0.900)
  Pallas kernels: 216 us -> 194 us
    pallas_call x1, Pallas kernels: 216 us -> 194 us  [per_device(): pl.pallas_call(functools.partial(fused_kernel, nseq, ntp, depth // resp_k...]
where the time goes in v1:
time: 199 us; the launch traced here: 197 us
  Pallas kernels  194 us (97%)
  local copies, waits for them, and re-layouts  3.16 us (2%)
    pallas_call x1, Pallas kernels, per_device(): pl.pallas_call(functools.partial(fused_kernel, nseq, ntp, depth // resp_k...  194 us

profile of v1, /device:TPU:28, one launch (start us, length us, event | category | flops | bytes accessed | tf_op | source)
XLA Modules:
  0.0 197.1 jit_solution(5366456840869887800)
XLA Ops:
  0.0 193.9 %shard_map.73 = bf16[1,512,2048]{2,1,0:T(8,128)(2,1)} custom-call(s32[4]{0:T(128)} %lens_ref.1, bf16[512,2048]{1,0:T(8,128)(2,1)} %q_ref.1, bf16[512,256]{1,0:T(8,128)(2,1)} %kr_ref.1, bf16[512,256]{1,0:T(8,128)(2,1)} %vr_ref.1, bf16[256,256]{1,0:T(8,128)(2,1)} %pk_ref.1, bf16[256,256]{1,0:T(8,128)(2,1)} %pv_ref.1, bf16[2048,2048]{1,0:T(8,128)(2,1)} %w_hbm.1), custom_call_target="tpu_custom_call" | custom-call | tf_op jit(solution)/shard_map/pallas_call | solution.py:497
  193.9 3.2 %copy.9 = bf16[512,2048]{1,0:T(8,128)(2,1)} copy(bf16[512,2048]{1,0:T(8,128)(2,1)} %bitcast.1) | data formatting | bytes 4194304

commit v2 on v1

--- a/solution.py
+++ b/solution.py
@@ -12,11 +12,15 @@
 LOG2E = 1.4426950408889634
 
 
-def attend_block(q, kp, vp, kr, vr, first, rows):
-    c = (HD ** -0.5) * LOG2E
+def scores(q, kp, kr):
     nt = (((1,), (1,)), ((), ()))
     sp = lax.dot_general(q, kp, nt, preferred_element_type=jnp.float32)
     sr = lax.dot_general(q, kr, nt, preferred_element_type=jnp.float32)
+    return sp, sr
+
+
+def attend(sp, sr, vp, vr, first, rows):
+    c = (HD ** -0.5) * LOG2E
     qpos = lax.broadcasted_iota(jnp.int32, sr.shape, 0) % rows + first
     kpos = lax.broadcasted_iota(jnp.int32, sr.shape, 1)
     sr = jnp.where(kpos <= qpos, sr, -1e30)
@@ -33,16 +37,20 @@
 
 MESH = pl.DeviceIdType.MESH
 WPIECES = 4
+PIECES = 4
+ORDER = (1, 2, 3, 0)
 NTILE = 512
-SCORES = 1 << 20
+SCORES = 3 << 18
+LAG_B = 1
+LAG_C = 3
 MLAG_A = MAXB + 1
-MLAG_C = MAXB + 5
+LATE = 2
 
 
 def fused_kernel(
     nseq, ntp, group,
     lens_ref, q_ref, kr_ref, vr_ref, pk_ref, pv_ref, w_hbm, out_ref,
-    pk_all, pv_all, w_ref, wm, ga, gb, part, half_in, quart_in, mig_in,
+    pk_all, pv_all, w_ref, wm, gath, part, half_in, quart_in, mig_in,
     p_send, p_recv, w_sem, wm_send, wm_recv, g_send, g_recv,
     a_send, a_recv, b_send, b_recv, f_send, f_recv, m_recv,
 ):
@@ -96,10 +104,9 @@
         )
 
     def g_copy(h, r, b, side):
-        buf = (ga, gb)[h]
-        return pltpu.make_async_remote_copy(
-            src_ref=buf.at[r, b],
-            dst_ref=buf.at[r, b],
+        return pltpu.make_async_remote_copy(
+            src_ref=gath.at[r, b, h],
+            dst_ref=gath.at[r, b, h],
             send_sem=g_send.at[h, side, r, b],
             recv_sem=g_recv.at[h, r, b],
             device_id={"seq": s - 1 + 2 * side},
@@ -162,6 +169,12 @@
         d = jnp.where(near, lax.div(j, twin) + 1, both + 1 + lax.div(jj, MAXB))
         b = jnp.where(near, lax.div(lax.rem(j, twin), 2), lax.rem(jj, MAXB))
         side = jnp.where(near, 2 * lax.rem(j, 2) - 1, far_side)
+        before = jnp.clip(lax.div(j - 2, 2), 0, MAXB)
+        outer = (j >= 3) & (j < 3 + twin) & (lax.rem(j, 2) == 1)
+        inner = j - before
+        side = jnp.where(is_pre, jnp.where(outer, -inward, inward), side)
+        d = jnp.where(is_pre, jnp.where(outer, 1, 1 + lax.div(inner, MAXB)), d)
+        b = jnp.where(is_pre, jnp.where(outer, before, lax.rem(inner, MAXB)), b)
         own = i < MAXB
         return jnp.where(own, s, s + side * d), jnp.where(own, i, b)
 
@@ -221,25 +234,23 @@
 
     loop(nseq, gather_prompt, 1)
 
+    def times(r, b, c, pieces):
+        y = 0.0
+        for h in pieces:
+            y = y + jnp.dot(
+                gath[r, b, h], w_ref[h * mig : (h + 1) * mig, c], preferred_element_type=jnp.float32
+            )
+        return y.astype(jnp.bfloat16)
+
     def project(i, r, b, full):
-        @pl.when(full)
-        def _():
-            def tile(j):
-                c = pl.ds(pl.multiple_of(j * NTILE, NTILE), NTILE)
-                y = jnp.dot(ga[r, b], w_ref[:mig, c], preferred_element_type=jnp.float32)
-                y = y + jnp.dot(gb[r, b], w_ref[mig:, c], preferred_element_type=jnp.float32)
-                part[i, :, c] = y.astype(jnp.bfloat16)
-
-            loop(cols // NTILE, tile)
-
-        @pl.when(jnp.logical_not(full))
-        def _():
-            def tile(j):
-                c = pl.ds(pl.multiple_of(j * NTILE, NTILE), NTILE)
-                y = jnp.dot(gb[r, b], w_ref[mig:, c], preferred_element_type=jnp.float32)
-                part[i, :, c] = y.astype(jnp.bfloat16)
-
-            loop(cols // NTILE, tile)
+        for ok, pieces in ((full, range(PIECES)), (jnp.logical_not(full), range(1, PIECES))):
+            @pl.when(ok)
+            def _():
+                def tile(j):
+                    c = pl.ds(pl.multiple_of(j * NTILE, NTILE), NTILE)
+                    part[i, :, c] = times(r, b, c, pieces)
+
+                loop(cols // NTILE, tile)
 
         a_copy(i).start()
 
@@ -249,45 +260,46 @@
         @pl.when(i < MAXB)
         def _():
             first = i * BLOCK
-            run = max(group // 2, 1)
+            heads = mig // HD
+            run = min(max(group // 2, 1), heads)
             while run % 2 == 0 and run * BLOCK * pk_all.shape[0] > SCORES:
                 run //= 2
-            sent = False
-            for k in range(kv_local):
-                kvc = slice(k * HD, (k + 1) * HD)
-                for h in range(k * group, (k + 1) * group, run):
-                    q = jnp.concatenate(
-                        [
-                            q_ref[pl.ds(first, BLOCK), (h + g) * HD : (h + g + 1) * HD]
-                            for g in range(run)
-                        ],
-                        axis=0,
-                    )
-                    o = attend_block(
-                        q, pk_all[:, kvc], pv_all[:, kvc], kr_ref[:, kvc], vr_ref[:, kvc],
-                        first, BLOCK,
-                    )
-                    for g in range(run):
-                        at = (h + g) * HD
-                        y = o[g * BLOCK : (g + 1) * BLOCK]
-                        if at < mig:
-                            ga[s, i, :, at : at + HD] = y
-                        else:
-                            gb[s, i, :, at - mig : at - mig + HD] = y
-                    if not sent and (h + run) * HD >= mig:
-                        sent = True
-                        send(0, s, i)
-            send(1, s, i)
+            runs = [h for p in ORDER for h in range(p * heads, (p + 1) * heads, run)]
+
+            def kv_cols(h):
+                return slice(h // group * HD, (h // group + 1) * HD)
+
+            def score(h):
+                q = jnp.concatenate(
+                    [
+                        q_ref[pl.ds(first, BLOCK), (h + g) * HD : (h + g + 1) * HD]
+                        for g in range(run)
+                    ],
+                    axis=0,
+                )
+                return scores(q, pk_all[:, kv_cols(h)], kr_ref[:, kv_cols(h)])
+
+            ready = score(runs[0])
+            for n, h in enumerate(runs):
+                now = ready
+                if n + 1 < len(runs):
+                    ready = score(runs[n + 1])
+                o = attend(*now, pv_all[:, kv_cols(h)], vr_ref[:, kv_cols(h)], first, BLOCK)
+                p = h // heads
+                for g in range(run):
+                    at = (h + g - p * heads) * HD
+                    gath[s, i, p, :, at : at + HD] = o[g * BLOCK : (g + 1) * BLOCK]
+                if h + run == (p + 1) * heads:
+                    send(p, s, i)
 
         @pl.when(i >= MAXB)
         def _():
-            @pl.when(jnp.logical_not(is_end))
-            def _():
-                g_copy(0, r, b, 0).wait_recv()
-
-            send(0, r, b)
-            g_copy(1, r, b, 0).wait_recv()
-            send(1, r, b)
+            for p in ORDER:
+                @pl.when(jnp.logical_not(is_end) | (p > 0))
+                def _():
+                    g_copy(p, r, b, 0).wait_recv()
+
+                send(p, r, b)
 
         @pl.when(i == 0)
         def _():
@@ -359,7 +371,7 @@
 
         def tile(j):
             c = pl.ds(pl.multiple_of(j * NTILE, NTILE), NTILE)
-            y = jnp.dot(ga[r, b], wm[:, c], preferred_element_type=jnp.float32)
+            y = jnp.dot(gath[r, b, 0], wm[:, c], preferred_element_type=jnp.float32)
             part[i, :, c] = y.astype(jnp.bfloat16)
 
         loop(cols // NTILE, tile)
@@ -373,36 +385,49 @@
         part[i, my_quart, :] = live(total + mig_in[m].astype(jnp.float32), r, b)
         deliver(i, r, b, end)
 
+    def between(i, low, count):
+        return (i >= low) & (i < low + count)
+
     def step(i):
         @pl.when(i < chunks)
         def _():
             stage_a(i)
 
-        @pl.when((i >= 1) & (i < chunks + 1))
-        def _():
-            stage_b(i - 1)
-
-        @pl.when((i >= 2) & (i < chunks + 2))
-        def _():
-            stage_c(i - 2)
-
-        @pl.when(is_pre & (i >= MLAG_A) & (i < MLAG_A + nmig))
+        @pl.when(between(i, LAG_B, chunks))
+        def _():
+            stage_b(i - LAG_B)
+
+        @pl.when(is_pre & between(i, MLAG_A, nmig))
         def _():
             mig_a(i - MLAG_A)
 
-        @pl.when(is_pre & (i >= MLAG_A + 1) & (i < MLAG_A + 1 + nmig))
-        def _():
-            stage_b(chunks + i - MLAG_A - 1)
-
-        @pl.when(is_pre & (i >= MLAG_C) & (i < MLAG_C + nmig))
-        def _():
-            mig_c(i - MLAG_C)
-
-    loop(max(chunks + 2, MLAG_C + nmig), step)
+        @pl.when(is_pre & between(i, MLAG_A + LAG_B, nmig))
+        def _():
+            stage_b(chunks + i - MLAG_A - LAG_B)
+
+        @pl.when(is_end & between(i, LAG_C, chunks))
+        def _():
+            stage_c(i - LAG_C)
+
+        def pairs(cond, count, fn):
+            @pl.when(cond & between(i, late, -(-count // 2)))
+            def _():
+                for k in range(2):
+                    n = 2 * (i - late) + k
+
+                    @pl.when(n < count)
+                    def _():
+                        fn(n)
+
+        pairs(jnp.logical_not(is_end), chunks, stage_c)
+        pairs(is_pre, nmig, mig_c)
+
+    late = chunks - LATE
+    loop(max(chunks + LAG_C, late + -(-chunks // 2)), step)
 
     def drain_send(i):
         r, b = chunk_of(i)
-        for h in range(2):
+        for h in range(PIECES):
             for side in (1, 0):
                 @pl.when(goes(h, r, side) & ((r == s) | jnp.logical_not(is_end)))
                 def _():
@@ -488,14 +513,16 @@
     nmig = (nseq - 1) * MAXB
     every = chunks + nmig
     cols = out_weight.shape[1]
-    mig = depth // HD // 4 * HD
+    mig = depth // PIECES
+    group = depth // resp_keys.shape[1]
+    assert mig % HD == 0 and group % (mig // HD) == 0
     prows, kvw = prompt_keys.shape
     quart = BLOCK // ntp
     bf = jnp.bfloat16
     dma = pltpu.SemaphoreType.DMA
     vmem = pl.BlockSpec(memory_space=pltpu.VMEM)
     out = pl.pallas_call(
-        functools.partial(fused_kernel, nseq, ntp, depth // resp_keys.shape[1]),
+        functools.partial(fused_kernel, nseq, ntp, group),
         out_shape=jax.ShapeDtypeStruct((per, rows, cols), bf),
         in_specs=[pl.BlockSpec(memory_space=pltpu.SMEM)]
         + [vmem] * 5
@@ -506,8 +533,7 @@
             pltpu.VMEM((nseq * prows, kvw), bf),
             pltpu.VMEM((depth, cols), bf),
             pltpu.VMEM((mig, cols), bf),
-            pltpu.VMEM((nseq, MAXB, BLOCK, mig), bf),
-            pltpu.VMEM((nseq, MAXB, BLOCK, depth - mig), bf),
+            pltpu.VMEM((nseq, MAXB, PIECES, BLOCK, mig), bf),
             pltpu.VMEM((every, BLOCK, cols), bf),
             pltpu.VMEM((every, BLOCK // 2, cols), bf),
             pltpu.VMEM((every, max(nx - 1, 1), quart, cols), bf),
@@ -517,8 +543,8 @@
             dma((WPIECES,)),
             dma((WPIECES,)),
             dma((WPIECES,)),
-            dma((2, 2, nseq, MAXB)),
-            dma((2, nseq, MAXB)),
+            dma((PIECES, 2, nseq, MAXB)),
+            dma((PIECES, nseq, MAXB)),
             dma((every,)),
             dma((every,)),
             dma((every, max(nx - 1, 1))),

time: 199 us -> 183 us (0.920)
  the two profiles are of different devices: /device:TPU:28 before, /device:TPU:1 now
where the time goes in v2:
time: 183 us
  Pallas kernels  180 us (98%)
  local copies, waits for them, and re-layouts  3.16 us (2%)
    pallas_call x1, Pallas kernels, per_device(): pl.pallas_call(functools.partial(fused_kernel, nseq, ntp, group), out_sha...  180 us

profile of v2, /device:TPU:1, one launch (start us, length us, event | category | flops | bytes accessed | tf_op | source)
XLA Modules:
  0.0 183.1 jit_solution(4142515995103465101)
XLA Ops:
  0.0 180.0 %shard_map.73 = bf16[1,512,2048]{2,1,0:T(8,128)(2,1)} custom-call(s32[4]{0:T(128)} %lens_ref.1, bf16[512,2048]{1,0:T(8,128)(2,1)} %q_ref.1, bf16[512,256]{1,0:T(8,128)(2,1)} %kr_ref.1, bf16[512,256]{1,0:T(8,128)(2,1)} %vr_ref.1, bf16[256,256]{1,0:T(8,128)(2,1)} %pk_ref.1, bf16[256,256]{1,0:T(8,128)(2,1)} %pv_ref.1, bf16[2048,2048]{1,0:T(8,128)(2,1)} %w_hbm.1), custom_call_target="tpu_custom_call" | custom-call | tf_op jit(solution)/shard_map/pallas_call | solution.py:524
  180.0 3.2 %copy.9 = bf16[512,2048]{1,0:T(8,128)(2,1)} copy(bf16[512,2048]{1,0:T(8,128)(2,1)} %bitcast.1) | data formatting | bytes 4194304

commit v3 on v2

--- a/solution.py
+++ b/solution.py
@@ -36,7 +36,6 @@
 
 
 MESH = pl.DeviceIdType.MESH
-WPIECES = 4
 PIECES = 4
 ORDER = (1, 2, 3, 0)
 NTILE = 512
@@ -44,14 +43,14 @@
 LAG_B = 1
 LAG_C = 3
 MLAG_A = MAXB + 1
-LATE = 2
+LATE = 1
 
 
 def fused_kernel(
     nseq, ntp, group,
-    lens_ref, q_ref, kr_ref, vr_ref, pk_ref, pv_ref, w_hbm, out_ref,
-    pk_all, pv_all, w_ref, wm, gath, part, half_in, quart_in, mig_in,
-    p_send, p_recv, w_sem, wm_send, wm_recv, g_send, g_recv,
+    lens_ref, pk_ref, pv_ref, q_hbm, kr_hbm, vr_hbm, w_hbm, out_ref,
+    q_ref, kr_ref, vr_ref, pk_all, pv_all, w_ref, wm, gath, part, half_in, quart_in, mig_in,
+    in_sem, p_send, p_recv, w_sem, wm_send, wm_recv, g_send, g_recv,
     a_send, a_recv, b_send, b_recv, f_send, f_recv, m_recv,
 ):
     s = lax.axis_index("seq")
@@ -76,38 +75,47 @@
     end = jnp.where(s < nseq // 2, 0, last)
     inward = jnp.where(s < nseq // 2, 1, -1)
 
+    def kind(i):
+        return jnp.where(i < chunks, 0, 1)
+
     def p_copy(r, side, kv, own=False):
         dst = (pk_all, pv_all)[kv]
         src = (pk_ref, pv_ref)[kv] if own else dst.at[pl.ds(r * prows, prows)]
         return pltpu.make_async_remote_copy(
             src_ref=src,
             dst_ref=dst.at[pl.ds(r * prows, prows)],
-            send_sem=p_send.at[side, r, kv],
-            recv_sem=p_recv.at[r, kv],
+            send_sem=p_send.at[side, r],
+            recv_sem=p_recv.at[r],
             device_id={"seq": s - 1 + 2 * side},
             device_id_type=MESH,
         )
 
-    def w_local(k):
-        rows = pl.ds(k * (depth // WPIECES), depth // WPIECES)
-        return pltpu.make_async_copy(w_hbm.at[rows], w_ref.at[rows], w_sem.at[k])
-
-    def w_copy(k):
-        rows = pl.ds(k * (mig // WPIECES), mig // WPIECES)
-        return pltpu.make_async_remote_copy(
-            src_ref=w_hbm.at[rows],
-            dst_ref=wm.at[rows],
-            send_sem=wm_send.at[k],
-            recv_sem=wm_recv.at[k],
-            device_id={"seq": jnp.where(is_end, s + inward, end)},
-            device_id_type=MESH,
-        )
+    def p_pair(r, side):
+        both_kinds = pk_all.at[pl.ds(0, 2 * prows)]
+        return pltpu.make_async_remote_copy(
+            src_ref=both_kinds,
+            dst_ref=both_kinds,
+            send_sem=p_send.at[side, r],
+            recv_sem=p_recv.at[r],
+            device_id={"seq": s - 1 + 2 * side},
+            device_id_type=MESH,
+        )
+
+    w_local = pltpu.make_async_copy(w_hbm, w_ref, w_sem)
+    w_copy = pltpu.make_async_remote_copy(
+        src_ref=w_hbm.at[pl.ds(0, mig)],
+        dst_ref=wm,
+        send_sem=wm_send,
+        recv_sem=wm_recv,
+        device_id={"seq": jnp.where(is_end, s + inward, end)},
+        device_id_type=MESH,
+    )
 
     def g_copy(h, r, b, side):
         return pltpu.make_async_remote_copy(
             src_ref=gath.at[r, b, h],
             dst_ref=gath.at[r, b, h],
-            send_sem=g_send.at[h, side, r, b],
+            send_sem=g_send.at[side, r],
             recv_sem=g_recv.at[h, r, b],
             device_id={"seq": s - 1 + 2 * side},
             device_id_type=MESH,
@@ -117,7 +125,7 @@
         return pltpu.make_async_remote_copy(
             src_ref=part.at[i, pl.ds((1 - core) * half, half)],
             dst_ref=half_in.at[i],
-            send_sem=a_send.at[i],
+            send_sem=a_send.at[kind(i)],
             recv_sem=a_recv.at[i],
             device_id={"tp": partner},
             device_id_type=MESH,
@@ -128,7 +136,7 @@
         return pltpu.make_async_remote_copy(
             src_ref=part.at[i, pl.ds(core * half + other * quart, quart)],
             dst_ref=quart_in.at[i, k - 1],
-            send_sem=b_send.at[i, k - 1],
+            send_sem=b_send.at[kind(i), k - 1],
             recv_sem=b_recv.at[i, k - 1],
             device_id={"tp": other * 2 + core},
             device_id_type=MESH,
@@ -142,8 +150,8 @@
         return pltpu.make_async_remote_copy(
             src_ref=part.at[i, my_quart],
             dst_ref=out_ref.at[slab, pl.ds(row_of(b), quart)],
-            send_sem=f_send.at[i],
-            recv_sem=f_recv.at[b, slab, t],
+            send_sem=f_send.at[kind(i)],
+            recv_sem=f_recv.at[slab],
             device_id={"seq": r, "tp": home},
             device_id_type=MESH,
         )
@@ -152,7 +160,7 @@
         return pltpu.make_async_remote_copy(
             src_ref=part.at[i, my_quart],
             dst_ref=mig_in.at[m],
-            send_sem=f_send.at[i],
+            send_sem=f_send.at[kind(i)],
             recv_sem=m_recv.at[m],
             device_id={"seq": jnp.where(is_end, s + inward, end)},
             device_id_type=MESH,
@@ -201,6 +209,27 @@
             def _():
                 g_copy(h, r, b, side).start()
 
+    inputs = [
+        pltpu.make_async_copy(src, dst, in_sem.at[k])
+        for k, (src, dst) in enumerate(((q_hbm, q_ref), (kr_hbm, kr_ref), (vr_hbm, vr_ref)))
+    ]
+    barrier = pltpu.get_barrier_semaphore()
+    peers = nseq * ntp
+
+    def greet(k):
+        other = lax.rem(s * ntp + t + k, peers)
+        pl.semaphore_signal(
+            barrier,
+            inc=1,
+            device_id={"seq": lax.div(other, ntp), "tp": lax.rem(other, ntp)},
+            device_id_type=MESH,
+        )
+
+    loop(peers, greet, 1)
+    for copy in inputs:
+        copy.start()
+    pl.semaphore_wait(barrier, peers - 1)
+
     for side, ok in ((0, has_left), (1, has_right)):
         @pl.when(ok)
         def _():
@@ -209,11 +238,9 @@
 
     @pl.when(is_end)
     def _():
-        for k in range(WPIECES):
-            w_copy(k).start()
-
-    for k in range(WPIECES):
-        w_local(k).start()
+        w_copy.start()
+
+    w_local.start()
 
     pk_all[pl.ds(s * prows, prows), :] = pk_ref[...]
     pv_all[pl.ds(s * prows, prows), :] = pv_ref[...]
@@ -225,14 +252,16 @@
         ):
             @pl.when(ok)
             def _():
-                for kv in range(2):
-                    p_copy(r, side, kv).wait_recv()
-
-                    @pl.when(onward)
-                    def _():
+                p_pair(r, side).wait_recv()
+
+                @pl.when(onward)
+                def _():
+                    for kv in range(2):
                         p_copy(r, side, kv).start()
 
     loop(nseq, gather_prompt, 1)
+    for copy in inputs:
+        copy.wait()
 
     def times(r, b, c, pieces):
         y = 0.0
@@ -303,8 +332,7 @@
 
         @pl.when(i == 0)
         def _():
-            for k in range(WPIECES):
-                w_local(k).wait()
+            w_local.wait()
 
         project(i, r, b, (i < MAXB) | jnp.logical_not(is_end))
 
@@ -366,8 +394,7 @@
 
         @pl.when(m == 0)
         def _():
-            for k in range(WPIECES):
-                w_copy(k).wait_recv()
+            w_copy.wait_recv()
 
         def tile(j):
             c = pl.ds(pl.multiple_of(j * NTILE, NTILE), NTILE)
@@ -405,7 +432,7 @@
         def _():
             stage_b(chunks + i - MLAG_A - LAG_B)
 
-        @pl.when(is_end & between(i, LAG_C, chunks))
+        @pl.when(between(i, LAG_C, jnp.where(is_end, chunks, MAXB)))
         def _():
             stage_c(i - LAG_C)
 
@@ -419,87 +446,74 @@
                     def _():
                         fn(n)
 
-        pairs(jnp.logical_not(is_end), chunks, stage_c)
+        pairs(jnp.logical_not(is_end), chunks - MAXB, lambda n: stage_c(n + MAXB))
         pairs(is_pre, nmig, mig_c)
 
     late = chunks - LATE
     loop(max(chunks + LAG_C, late + -(-chunks // 2)), step)
 
-    def drain_send(i):
-        r, b = chunk_of(i)
-        for h in range(PIECES):
-            for side in (1, 0):
-                @pl.when(goes(h, r, side) & ((r == s) | jnp.logical_not(is_end)))
-                def _():
-                    g_copy(h, r, b, side).wait_send()
-
-        a_copy(i).wait_send()
-        for k in range(1, nx):
-            b_copy(i, k).wait_send()
-
-        @pl.when(hands_over(r))
-        def _():
-            m_copy(i, i - MAXB).wait_send()
-
-        @pl.when(jnp.logical_not(hands_over(r) | stays(r, s)))
-        def _():
-            f_copy(i, r, b, s).wait_send()
-
-    loop(chunks, drain_send)
-
-    @pl.when(is_pre)
-    def _():
-        def drain_mig(m):
-            r, b = mig_of(m)
-            i = chunks + m
-            a_copy(i).wait_send()
+    def drain(ref, send_sem=None, recv_sem=None):
+        return pltpu.make_async_remote_copy(
+            src_ref=ref,
+            dst_ref=ref,
+            send_sem=f_send.at[0] if send_sem is None else send_sem,
+            recv_sem=f_recv.at[0] if recv_sem is None else recv_sem,
+            device_id={"tp": partner},
+            device_id_type=MESH,
+        )
+
+    def drain_gathered(r):
+        for side, ok, whole in (
+            (1, has_right & (r <= s), s + 1 < last),
+            (0, has_left & (r >= s), s > 1),
+        ):
+            @pl.when(ok & whole)
+            def _():
+                drain(gath.at[r], g_send.at[side, r]).wait_send()
+
+            @pl.when(ok & jnp.logical_not(whole))
+            def _():
+                drain(gath.at[r, :, pl.ds(1, PIECES - 1)], g_send.at[side, r]).wait_send()
+
+            @pl.when(ok)
+            def _():
+                p_pair(r, side).wait_send()
+
+    loop(nseq, drain_gathered)
+
+    for n, low, count, cond, owner in (
+        (0, 0, chunks, None, s),
+        (1, chunks, nmig, is_pre, end),
+    ):
+        local = lax.div(owner, per) == t
+        yes = s >= 0 if cond is None else cond
+
+        @pl.when(yes)
+        def _():
+            drain(half_in.at[pl.ds(low, count)], a_send.at[n]).wait_send()
             for k in range(1, nx):
-                b_copy(i, k).wait_send()
-
-            @pl.when(jnp.logical_not(stays(r, end)))
-            def _():
-                f_copy(i, r, b, end).wait_send()
-
-        loop(nmig, drain_mig)
+                drain(quart_in.at[pl.ds(low, count), k - 1], b_send.at[n, k - 1]).wait_send()
+
+        for here in (True, False):
+            @pl.when(yes & (local if here else jnp.logical_not(local)))
+            def _():
+                sent = count - MAXB if here else count
+                drain(part.at[pl.ds(low, sent), pl.ds(0, quart)], f_send.at[n]).wait_send()
 
     @pl.when(is_end)
     def _():
-        for k in range(WPIECES):
-            w_copy(k).wait_send()
-
-    def drain_prompt(r):
-        for kv in range(2):
-            @pl.when(has_right & (r <= s))
-            def _():
-                p_copy(r, 1, kv).wait_send()
-
-            @pl.when(has_left & (r >= s))
-            def _():
-                p_copy(r, 0, kv).wait_send()
-
-    loop(nseq, drain_prompt)
-
-    def drain_out(m):
-        b = lax.div(m, per * ntp)
-        j = lax.div(lax.rem(m, per * ntp), ntp)
-        u = lax.rem(m, ntp)
+        w_copy.wait_send()
+
+    for j in range(per):
         owner = t * per + j
         far = owner != s
         origin = jnp.where(far & (owner == 0), 1, jnp.where(far & (owner == last), last - 1, owner))
-
-        @pl.when(jnp.logical_not((origin == s) & (u == t)))
-        def _():
-            row = b * BLOCK + lax.rem(u, 2) * half + lax.div(u, 2) * quart
-            pltpu.make_async_remote_copy(
-                src_ref=part.at[0, my_quart],
-                dst_ref=out_ref.at[j, pl.ds(row, quart)],
-                send_sem=f_send.at[0],
-                recv_sem=f_recv.at[b, j, u],
-                device_id={"seq": s, "tp": partner},
-                device_id_type=MESH,
-            ).wait_recv()
-
-    loop(MAXB * per * ntp, drain_out)
+        rows = out_ref.shape[1]
+        for here in (True, False):
+            @pl.when(origin == s if here else origin != s)
+            def _():
+                count = rows - MAXB * quart if here else rows
+                drain(out_ref.at[j, pl.ds(0, count)], recv_sem=f_recv.at[j]).wait_recv()
 
 
 def per_device(
@@ -525,10 +539,13 @@
         functools.partial(fused_kernel, nseq, ntp, group),
         out_shape=jax.ShapeDtypeStruct((per, rows, cols), bf),
         in_specs=[pl.BlockSpec(memory_space=pltpu.SMEM)]
-        + [vmem] * 5
-        + [pl.BlockSpec(memory_space=pl.ANY)],
+        + [vmem] * 2
+        + [pl.BlockSpec(memory_space=pl.ANY)] * 4,
         out_specs=vmem,
         scratch_shapes=[
+            pltpu.VMEM(resp_queries.shape, bf),
+            pltpu.VMEM(resp_keys.shape, bf),
+            pltpu.VMEM(resp_values.shape, bf),
             pltpu.VMEM((nseq * prows, kvw), bf),
             pltpu.VMEM((nseq * prows, kvw), bf),
             pltpu.VMEM((depth, cols), bf),
@@ -538,25 +555,26 @@
             pltpu.VMEM((every, BLOCK // 2, cols), bf),
             pltpu.VMEM((every, max(nx - 1, 1), quart, cols), bf),
             pltpu.VMEM((nmig, quart, cols), bf),
-            dma((2, nseq, 2)),
-            dma((nseq, 2)),
-            dma((WPIECES,)),
-            dma((WPIECES,)),
-            dma((WPIECES,)),
-            dma((PIECES, 2, nseq, MAXB)),
+            dma((3,)),
+            dma((2, nseq)),
+            dma((nseq,)),
+            dma,
+            dma,
+            dma,
+            dma((2, nseq)),
             dma((PIECES, nseq, MAXB)),
+            dma((2,)),
             dma((every,)),
-            dma((every,)),
+            dma((2, max(nx - 1, 1))),
             dma((every, max(nx - 1, 1))),
-            dma((every, max(nx - 1, 1))),
-            dma((every,)),
-            dma((MAXB, per, ntp)),
+            dma((2,)),
+            dma((per,)),
             dma((nmig,)),
         ],
         compiler_params=pltpu.CompilerParams(
-            has_side_effects=True, vmem_limit_bytes=61000 * 1024
+            has_side_effects=True, collective_id=0, vmem_limit_bytes=61000 * 1024
         ),
-    )(resp_blocks, resp_queries, resp_keys, resp_values, prompt_keys, prompt_values, out_weight)
+    )(resp_blocks, prompt_keys, prompt_values, resp_queries, resp_keys, resp_values, out_weight)
     return out.transpose(1, 0, 2).reshape(rows, per * cols)
 
 

time: 183 us -> 168 us (0.918)
  the two profiles are of different devices: /device:TPU:1 before, /device:TPU:28 now
where the time goes in v3:
time: 168 us; the launch traced here: 165 us
  Pallas kernels  162 us (96%)
  local copies, waits for them, and re-layouts  3.16 us (2%)
    pallas_call x1, Pallas kernels, per_device(): pl.pallas_call(functools.partial(fused_kernel, nseq, ntp, group), out_sha...  162 us

profile of v3, /device:TPU:28, one launch (start us, length us, event | category | flops | bytes accessed | tf_op | source)
XLA Modules:
  0.0 165.4 jit_solution(4923498291042774104)
XLA Ops:
  0.0 162.3 %shard_map.73 = bf16[1,512,2048]{2,1,0:T(8,128)(2,1)} custom-call(s32[4]{0:T(128)} %lens_ref.1, bf16[256,256]{1,0:T(8,128)(2,1)} %pk_ref.1, bf16[256,256]{1,0:T(8,128)(2,1)} %pv_ref.1, bf16[512,2048]{1,0:T(8,128)(2,1)} %q_hbm.1, bf16[512,256]{1,0:T(8,128)(2,1)} %kr_hbm.1, bf16[512,256]{1,0:T(8,128)(2,1)} %vr_hbm.1, bf16[2048,2048]{1,0:T(8,128)(2,1)} %w_hbm.1), custom_call_target="tpu_custom_call" | custom-call | tf_op jit(solution)/shard_map/pallas_call | solution.py:538
  162.3 3.2 %copy.9 = bf16[512,2048]{1,0:T(8,128)(2,1)} copy(bf16[512,2048]{1,0:T(8,128)(2,1)} %bitcast.1) | data formatting | bytes 4194304

commit v4 on v3

--- a/solution.py
+++ b/solution.py
@@ -85,7 +85,7 @@
             src_ref=src,
             dst_ref=dst.at[pl.ds(r * prows, prows)],
             send_sem=p_send.at[side, r],
-            recv_sem=p_recv.at[r],
+            recv_sem=p_recv.at[r, kv],
             device_id={"seq": s - 1 + 2 * side},
             device_id_type=MESH,
         )
@@ -96,14 +96,14 @@
             src_ref=both_kinds,
             dst_ref=both_kinds,
             send_sem=p_send.at[side, r],
-            recv_sem=p_recv.at[r],
+            recv_sem=p_recv.at[r, 0],
             device_id={"seq": s - 1 + 2 * side},
             device_id_type=MESH,
         )
 
     w_local = pltpu.make_async_copy(w_hbm, w_ref, w_sem)
     w_copy = pltpu.make_async_remote_copy(
-        src_ref=w_hbm.at[pl.ds(0, mig)],
+        src_ref=w_ref.at[pl.ds(0, mig)],
         dst_ref=wm,
         send_sem=wm_send,
         recv_sem=wm_recv,
@@ -226,6 +226,7 @@
         )
 
     loop(peers, greet, 1)
+    w_local.start()
     for copy in inputs:
         copy.start()
     pl.semaphore_wait(barrier, peers - 1)
@@ -236,11 +237,12 @@
             p_copy(s, side, 0, own=True).start()
             p_copy(s, side, 1, own=True).start()
 
+    w_local.wait()
+
     @pl.when(is_end)
     def _():
         w_copy.start()
 
-    w_local.start()
 
     pk_all[pl.ds(s * prows, prows), :] = pk_ref[...]
     pv_all[pl.ds(s * prows, prows), :] = pv_ref[...]
@@ -252,11 +254,11 @@
         ):
             @pl.when(ok)
             def _():
-                p_pair(r, side).wait_recv()
-
-                @pl.when(onward)
-                def _():
-                    for kv in range(2):
+                for kv in range(2):
+                    p_copy(r, side, kv).wait_recv()
+
+                    @pl.when(onward)
+                    def _():
                         p_copy(r, side, kv).start()
 
     loop(nseq, gather_prompt, 1)
@@ -330,10 +332,6 @@
 
                 send(p, r, b)
 
-        @pl.when(i == 0)
-        def _():
-            w_local.wait()
-
         project(i, r, b, (i < MAXB) | jnp.logical_not(is_end))
 
     def stage_b(i):
@@ -514,6 +512,28 @@
             def _():
                 count = rows - MAXB * quart if here else rows
                 drain(out_ref.at[j, pl.ds(0, count)], recv_sem=f_recv.at[j]).wait_recv()
+
+
+def place_kernel(steps, src, dst, held, in_sem, out_sem):
+    per, rows, cols = src.shape
+    tall = rows // steps
+
+    def pair(j, k):
+        at = pl.ds(k * tall, tall)
+        there = dst.at[at, pl.ds(j * cols, cols)]
+        return (
+            pltpu.make_async_copy(src.at[j, at], held.at[j, at], in_sem.at[j, k]),
+            pltpu.make_async_copy(held.at[j, at], there, out_sem.at[j, k]),
+        )
+
+    every = [pair(j, k) for j in range(per) for k in range(steps)]
+    for first, _ in every:
+        first.start()
+    for first, second in every:
+        first.wait()
+        second.start()
+    for _, second in every:
+        second.wait()
 
 
 def per_device(
@@ -557,7 +577,7 @@
             pltpu.VMEM((nmig, quart, cols), bf),
             dma((3,)),
             dma((2, nseq)),
-            dma((nseq,)),
+            dma((nseq, 2)),
             dma,
             dma,
             dma,
@@ -575,7 +595,14 @@
             has_side_effects=True, collective_id=0, vmem_limit_bytes=61000 * 1024
         ),
     )(resp_blocks, prompt_keys, prompt_values, resp_queries, resp_keys, resp_values, out_weight)
-    return out.transpose(1, 0, 2).reshape(rows, per * cols)
+    steps = 8
+    return pl.pallas_call(
+        functools.partial(place_kernel, steps),
+        out_shape=jax.ShapeDtypeStruct((rows, per * cols), bf),
+        in_specs=[pl.BlockSpec(memory_space=pl.ANY)],
+        out_specs=pl.BlockSpec(memory_space=pl.ANY),
+        scratch_shapes=[pltpu.VMEM((per, rows, cols), bf), dma((per, steps)), dma((per, steps))],
+    )(out)
 
 
 def solution(mesh):

time: 168 us -> 166 us (0.988)
  local copies, waits for them, and re-layouts: 3.16 us -> 0 us
  Pallas kernels: 162 us -> 165 us
    unnamed x1 -> x0, local copies, waits for them, and re-layouts: 3.16 us -> none
    pallas_call x0 -> x1, Pallas kernels: none -> 2.39 us  [per_device(): pl.pallas_call(functools.partial(place_kernel, steps), out_shape=jax.Shap...]
where the time goes in v4:
time: 166 us; the launch traced here: 165 us
  Pallas kernels  165 us (99%)
    pallas_call x1, Pallas kernels, per_device(): pl.pallas_call(functools.partial(fused_kernel, nseq, ntp, group), out_sha...  163 us

profile of v4, /device:TPU:28, one launch (start us, length us, event | category | flops | bytes accessed | tf_op | source)
XLA Modules:
  0.0 165.0 jit_solution(13779196669897253745)
XLA Ops:
  0.0 162.6 %shard_map.73.src = bf16[1,512,2048]{2,1,0:T(8,128)(2,1)} custom-call(s32[4]{0:T(128)} %lens_ref.1, bf16[256,256]{1,0:T(8,128)(2,1)} %pk_ref.1, bf16[256,256]{1,0:T(8,128)(2,1)} %pv_ref.1, bf16[512,2048]{1,0:T(8,128)(2,1)} %q_hbm.1, bf16[512,256]{1,0:T(8,128)(2,1)} %kr_hbm.1, bf16[512,256]{1,0:T(8,128)(2,1)} %vr_hbm.1, bf16[2048,2048]{1,0:T(8,128)(2,1)} %w_hbm.1), custom_call_target="tpu_custom_call" | custom-call | tf_op jit(solution)/shard_map/pallas_call | solution.py:558
  162.6 2.4 %shard_map.74 = bf16[512,2048]{1,0:T(8,128)(2,1)} custom-call(bf16[1,512,2048]{2,1,0:T(8,128)(2,1)} %shard_map.73.src), custom_call_target="tpu_custom_call" | custom-call | tf_op jit(solution)/shard_map/pallas_call | solution.py:599
